TPU v7x, 256 devices: a whole 4x4x8 slice. The times are simulated.
256 devices in a mesh: expert: 8 (over x, y_lo), tensor: 16 (over y_hi, z), dp: 2 (over core).
Axes of the slice: x: 4, y: 4 (y_hi: 2, y_lo: 2; y = y_hi * 2 + y_lo), z: 8, core: 2. Of those that a mesh axis runs over, the one named last changes fastest.
Arguments:
- x_real: bfloat16 [4096, 2048], P(('expert', 'dp'), 'tensor'), may hold values from -6 to 6
- routes_real: int32 [4096, 2], P(('expert', 'dp')), may hold values from 0 to 7, all different within a row; in each aligned block of 256 rows (0 to 255, 256 to 511, ...) at most 128 rows name the same one
- gates_real: float32 [4096, 2], P(('expert', 'dp')), may hold values from 0.2 to 1
- up_real: bfloat16 [8, 2048, 8192], P('expert', None, 'tensor'), may hold values from -0.125 to 0.125
- down_real: bfloat16 [8, 8192, 2048], P('expert', 'tensor'), may hold values from -0.0625 to 0.0625
- x_fake: bfloat16 [4096, 2048], P(('expert', 'dp'), 'tensor'), may hold values from -6 to 6
- routes_fake: int32 [4096, 2], P(('expert', 'dp')), may hold values from 0 to 7, all different within a row; in each aligned block of 256 rows (0 to 255, 256 to 511, ...) at most 128 rows name the same one
- gates_fake: float32 [4096, 2], P(('expert', 'dp')), may hold values from 0.2 to 1
- cotangent: bfloat16 [4096, 2048], P(('expert', 'dp'), 'tensor'), may hold values from -6 to 6
- up_fake: bfloat16 [8, 2048, 8192], P('expert', None, 'tensor'), may hold values from -0.125 to 0.125
- down_fake: bfloat16 [8, 8192, 2048], P('expert', 'tensor'), may hold values from -0.0625 to 0.0625
Outputs:
- real_out: bfloat16 [4096, 2048], P(('expert', 'dp'), 'tensor')
- grad_up: bfloat16 [8, 2048, 8192], P('expert', 'dp', 'tensor')
- grad_down: bfloat16 [8, 8192, 2048], P('expert', 'tensor', 'dp')
Inputs may be any that keep to these rules, and one draw needn't show every extreme that they name: `routes_real`: each row names 2 different experts. In the 256 rows of one index of expert and dp no expert is named more than 128 times, and that bound is reached. `routes_fake`: each row names 2 different experts. In the 256 rows of one index of expert and dp no expert is named more than 128 times, and that bound is reached.
All inputs are finite; a program needn't handle non-finite values.
Results may differ from a plain program's by a relative error of at most 0.0058.
Values may be sent and summed in bfloat16 or wider, within the bound.
A program may use at most 128 MiB of HBM per device.

v0:
```python
import jax
import jax.numpy as jnp
from jax import lax
from jax.sharding import Mesh
from jax.sharding import PartitionSpec as P

TENSOR = ("tensor_0", "tensor_1")
slope_const = 0.7978845608028654
cubic_coef = 0.044715


def in_order(pieces, dim):
    pieces = jnp.moveaxis(pieces, 0, dim)
    dims = pieces.shape
    return pieces.reshape(*dims[:dim], dims[dim] * dims[dim + 1], *dims[dim + 2 :])


def sent_to_all(x, axis):
    copies = jnp.broadcast_to(x, (lax.axis_size(axis), *x.shape))
    return lax.all_to_all(copies, axis, split_axis=0, concat_axis=0, tiled=True)


def gather_directly(x, axis, dim):
    return in_order(sent_to_all(x, axis), dim)


def reduced_to_own(pieces, axes, turns):
    dims = [lax.axis_size(a) for a in axes]
    pieces = pieces.reshape(*dims, *pieces.shape[1:])
    pieces = pieces.transpose(*turns, *range(len(axes), pieces.ndim))
    pieces = pieces.reshape(-1, *pieces.shape[len(axes) :])
    for k in turns:
        pieces = lax.psum_scatter(pieces, axes[k], scatter_dimension=0, tiled=True)
    return pieces[0]


def in_blocks(x, dim, length):
    dims = x.shape
    pieces = x.reshape(*dims[:dim], length, dims[dim] // length, *dims[dim + 1 :])
    return jnp.moveaxis(pieces, dim, 0)


def sum_by_axis(x, axes, turns, dim):
    length = lax.axis_size(axes)
    return reduced_to_own(in_blocks(x, dim, length), axes, turns)


def sent_together(arrays, axis, dim, along):
    ends, at = ([], 0)
    for a in arrays[:-1]:
        at += a.shape[along]
        ends.append(at)
    both = jnp.concatenate(arrays, axis=along)
    return tuple(jnp.split(lax.all_gather(both, axis, axis=dim, tiled=True), ends, axis=along))


def in_one_piece(arrays, axis, split_dim, concat_dim, along):
    ends, at = ([], 0)
    for a in arrays[:-1]:
        at += a.shape[along]
        ends.append(at)
    both = jnp.concatenate(arrays, axis=along)
    return tuple(
        jnp.split(
            lax.all_to_all(both, axis, split_axis=split_dim, concat_axis=concat_dim, tiled=True),
            ends,
            axis=along,
        )
    )


def partner(value, axis, stride):
    mask = 2**stride
    pairs = [(source, source ^ mask) for source in range(lax.axis_size(axis))]
    return lax.ppermute(value, axis, pairs)


def gelu_tanh(value):
    return (
        0.5 * value * (1.0 + jnp.tanh(slope_const * (value + cubic_coef * value * value * value)))
    )


def gelu_slope(value):
    inner = jnp.tanh(slope_const * (value + cubic_coef * value * value * value))
    return 0.5 * (1.0 + inner) + 0.5 * value * (1.0 - inner * inner) * slope_const * (
        1.0 + 3.0 * cubic_coef * value * value
    )


def slot_index(routes, experts, capacity):
    labels = jnp.arange(experts, dtype=jnp.int32)
    hits = (routes[:, :, None] == labels[None, None, :]).astype(jnp.int32)
    per_token = jnp.sum(hits, axis=1)
    before = jnp.cumsum(per_token, axis=0) - per_token
    slots = jnp.sum(hits * before[:, None, :], axis=2)
    return routes * capacity + slots


def spread_matrix(position, total):
    columns = jnp.arange(total, dtype=jnp.int32)
    match = (position[:, :, None] == columns[None, None, :]).astype(jnp.float32)
    return jnp.sum(match, axis=1).astype(jnp.bfloat16)


def pick_matrix(position, total):
    columns = jnp.arange(total, dtype=jnp.int32)
    flat = position.reshape(-1)
    return (flat[:, None] == columns[None, :]).astype(jnp.bfloat16)


def to_slots(matrix, rows):
    return lax.dot_general(
        matrix, rows, (((0,), (0,)), ((), ())), preferred_element_type=jnp.float32
    )


def over_rows(left, right):
    return lax.dot_general(
        left, right, (((0,), (0,)), ((), ())), preferred_element_type=jnp.float32
    )


def scale_rows(gates, rows):
    scaled = gates[:, :, None] * rows[:, None, :].astype(jnp.float32)
    return scaled.astype(jnp.bfloat16).reshape(-1, rows.shape[1])


def on_device(
    x_real,
    routes_real,
    gates_real,
    up_real,
    down_real,
    x_fake,
    routes_fake,
    gates_fake,
    cotangent,
    up_fake,
    down_fake,
):
    experts = lax.axis_size("expert")
    tokens = x_real.shape[0]
    top = routes_real.shape[1]
    capacity = tokens // 2
    total = experts * capacity
    w_up = up_real[0]
    w_down = down_real[0]
    wf_up = up_fake[0]
    wf_down = down_fake[0]
    real_pos = slot_index(routes_real, experts, capacity)
    real_pick = spread_matrix(real_pos, total)
    whole = lax.all_gather(x_real, TENSOR, axis=1, tiled=True)
    fake_pos = slot_index(routes_fake, experts, capacity)
    fake_pick = spread_matrix(fake_pos, total)
    fake_flat = pick_matrix(fake_pos, total)
    part = x_fake.shape[1]
    sent_x = to_slots(fake_pick, x_fake).astype(jnp.bfloat16).reshape(experts, capacity, part)
    sent_d = (
        to_slots(fake_flat, scale_rows(gates_fake, cotangent))
        .astype(jnp.bfloat16)
        .reshape(experts, capacity, part)
    )
    got_x, got_d = in_one_piece((sent_x, sent_d), "expert", 0, 0, 1)
    both = jnp.concatenate((got_x.reshape(total, part), got_d.reshape(total, part)), axis=0)
    whole, both = lax.optimization_barrier((whole, both))
    both = lax.all_gather(both, TENSOR, axis=1, tiled=True)
    rows_x, rows_d = (both[:total], both[total:])
    width = whole.shape[1]
    sent = to_slots(real_pick, whole).astype(jnp.bfloat16).reshape(experts, capacity, width)
    arrived = lax.all_to_all(sent, "expert", split_axis=0, concat_axis=0, tiled=True)
    rows = arrived.reshape(total, width)
    pre_real = jnp.dot(rows, w_up, preferred_element_type=jnp.float32)
    hidden = gelu_tanh(pre_real).astype(jnp.bfloat16)
    partial_out = jnp.dot(hidden, w_down, preferred_element_type=jnp.float32).astype(jnp.bfloat16)
    returned = lax.all_to_all(
        partial_out.reshape(experts, capacity, width),
        "expert",
        split_axis=0,
        concat_axis=0,
        tiled=True,
    ).reshape(total, width)
    columns = jnp.arange(total, dtype=jnp.int32)
    match = (real_pos[:, :, None] == columns[None, None, :]).astype(jnp.float32)
    weights = jnp.sum(match * gates_real[:, :, None], axis=1)
    high = weights.astype(jnp.bfloat16)
    low = (weights - high.astype(jnp.float32)).astype(jnp.bfloat16)
    combined = jnp.dot(high, returned, preferred_element_type=jnp.float32) + jnp.dot(
        low, returned, preferred_element_type=jnp.float32
    )
    real_out = sum_by_axis(combined, TENSOR, (1, 0), 1).astype(jnp.bfloat16)
    pre_fake = jnp.dot(rows_x, wf_up, preferred_element_type=jnp.float32)
    act = gelu_tanh(pre_fake).astype(jnp.bfloat16)
    back_act = lax.dot_general(
        rows_d, wf_down, (((1,), (1,)), ((), ())), preferred_element_type=jnp.float32
    )
    dpre = (back_act * gelu_slope(pre_fake)).astype(jnp.bfloat16)
    mine = lax.axis_index("dp")
    half = rows_x.shape[1] // 2
    own_x = lax.dynamic_slice_in_dim(rows_x, mine * half, half, 1)
    other_x = lax.dynamic_slice_in_dim(rows_x, (1 - mine) * half, half, 1)
    own_d = lax.dynamic_slice_in_dim(rows_d, mine * half, half, 1)
    other_d = lax.dynamic_slice_in_dim(rows_d, (1 - mine) * half, half, 1)
    peer_x, peer_d, peer_act, peer_dpre = partner((other_x, other_d, act, dpre), "dp", 0)
    grad_in = over_rows(own_x, dpre) + over_rows(peer_x, peer_dpre)
    grad_out = over_rows(act, own_d) + over_rows(peer_act, peer_d)
    return (real_out, grad_in.astype(jnp.bfloat16)[None], grad_out.astype(jnp.bfloat16)[None])


def solution(mesh):
    split = Mesh(
        mesh.devices.reshape(mesh.shape["expert"], 2, 8, mesh.shape["dp"]),
        ("expert", "tensor_0", "tensor_1", "dp"),
    )
    placed = (
        P(("expert", "dp"), TENSOR),
        P(("expert", "dp"), None),
        P(("expert", "dp"), None),
        P("expert", None, TENSOR),
        P("expert", TENSOR, None),
        P(("expert", "dp"), TENSOR),
        P(("expert", "dp"), None),
        P(("expert", "dp"), None),
        P(("expert", "dp"), TENSOR),
        P("expert", None, TENSOR),
        P("expert", TENSOR, None),
    )
    return jax.shard_map(
        on_device,
        mesh=split,
        in_specs=placed,
        out_specs=(
            P(("expert", "dp"), TENSOR),
            P("expert", "dp", TENSOR),
            P("expert", TENSOR, "dp"),
        ),
        check_vma=False,
    )
```

profile of v0, /device:TPU:1, one launch (start us, length us, event | category | flops | bytes accessed | tf_op | source)
XLA Modules:
  0.0 432.8 jit_solution(8961847231231430238)
XLA Ops:
  7.2 0.7 all-gather.3.cloned.1.call-update
  7.9 0.7 convert_reduce_fusion.2
  8.6 0.6 reduce-window.16
  9.2 0.2 slice_reduce_fusion
  9.5 0.7 select_reduce_fusion.1
  10.2 0.7 multiply_add_fusion.2
  10.9 0.1 copy.30
  11.1 0.1 eq.86
  11.2 0.8 copy.31
  12.0 0.1 mul.132
  12.2 0.9 mul.134
  13.1 0.9 fusion.31
  14.0 0.3 convert_reduce_fusion
  14.3 0.3 convolution_convert_fusion.2
  14.6 0.8 pad_maximum_fusion
  15.5 5.8 %all-to-all-start = ((bf16[8,256,128]{2,1,0:T(8,128)(2,1)}), bf16[8,256,128]{2,1,0:T(8,128)(2,1)}, u32[]{:S(2)}, u32[]{:S(2)}) async-start(bf16[8,256,128]{2,1,0:T(8,128)(2,1)} %pad_maximum_fusion), calls=%async_computation | async-start | bytes 1048576 | tf_op jit(solution)/shard_map/all_to_all | solution.py:65
  21.4 0.6 reduce-window.14
  22.0 0.2 slice_reduce_fusion.1
  22.2 0.1 bitcast_subtract_fusion.1
  22.3 1.2 select_reduce_fusion
  23.6 6.0 %all-to-all-done = bf16[8,256,128]{2,1,0:T(8,128)(2,1)} async-done(((bf16[8,256,128]{2,1,0:T(8,128)(2,1)}), bf16[8,256,128]{2,1,0:T(8,128)(2,1)}, u32[]{:S(2)}, u32[]{:S(2)}) %all-to-all-start) | async-done | bytes 524320 | tf_op jit(solution)/shard_map/all_to_all | solution.py:65
  29.6 1.1 fusion.50
  30.7 0.8 pad_maximum_fusion.1
  31.5 55.5 %all-gather.3.cloned.1.call-done = bf16[256,2048]{1,0:T(8,128)(2,1)} async-done(((bf16[256,128]{1,0:T(8,128)(2,1)}), bf16[256,2048]{1,0:T(8,128)(2,1)}) %all-gather.3.cloned.1.call-update) | async-done | bytes 1048592 | tf_op jit(solution)/shard_map/all_gather | solution.py:153
  87.0 2.7 convolution_convert_fusion.1
  89.7 48.2 %all_to_all.15 = bf16[8,128,2048]{2,1,0:T(8,128)(2,1)} all-to-all(bf16[8,128,2048]{2,1,0:T(8,128)(2,1)S(1)} %bitcast.72), channel_id=1, replica_groups=mesh['expert'=8,'tensor_0'=2,'tensor_1'=8,'dp'=2] {'expert'}, dimensions={0} | all-to-all | bytes 8388608 | tf_op jit(solution)/shard_map/all_to_all | solution.py:171
  137.9 9.6 %convolution_convert_fusion = bf16[1024,2048]{1,0:T(8,128)(2,1)} fusion(bf16[1,512,2048]{2,1,0:T(8,128)(2,1)S(1)} %copy-done, bf16[1024,2048]{1,0:T(8,128)(2,1)} %bitcast.77, bf16[1,2048,512]{2,1,0:T(8,128)(2,1)} %param.14), kind=kOutput, calls=%fused_computation | convolution fusion | flops 4301783040 | bytes 12582912 | tf_op jit(solution)/shard_map/dot_general | solution.py:175
  147.5 46.6 %all_to_all.16 = bf16[8,128,2048]{2,1,0:T(8,128)(2,1)S(1)} all-to-all(bf16[8,128,2048]{2,1,0:T(8,128)(2,1)} %bitcast.78), channel_id=1, replica_groups=mesh['expert'=8,'tensor_0'=2,'tensor_1'=8,'dp'=2] {'expert'}, dimensions={0} | all-to-all | bytes 8388608 | tf_op jit(solution)/shard_map/all_to_all | solution.py:176
  194.1 1.3 fusion.38
  195.4 1.3 fusion.24
  196.7 0.4 copy.33
  197.1 2.0 copy.32
  199.2 0.7 all-gather.5.cloned.1.call-update
  200.0 39.7 %reduce-scatter.3.cloned.1.call-done = f32[2,256,128]{2,1,0:T(8,128)} async-done(((f32[16,256,128]{2,1,0:T(8,128)}), f32[2,256,128]{2,1,0:T(8,128)}) %reduce-scatter.3.cloned.1.call-update) | async-done | bytes 262160 | tf_op jit(solution)/shard_map/reduce_scatter | solution.py:33
  239.7 149.7 %all-gather.5.cloned.1.call-done = bf16[2048,2048]{1,0:T(8,128)(2,1)} async-done(((bf16[2048,128]{1,0:T(8,128)(2,1)}), bf16[2048,2048]{1,0:T(8,128)(2,1)}) %all-gather.5.cloned.1.call-update) | async-done | bytes 8388624 | tf_op jit(solution)/shard_map/all_gather | solution.py:167
  389.5 4.1 fusion.49
  393.6 0.2 constant_dynamic-slice_fusion.1
  393.9 4.4 %collective-permute-start = (bf16[1024,1024]{1,0:T(8,128)(2,1)S(1)}, bf16[1024,1024]{1,0:T(8,128)(2,1)}, u32[]{:S(2)}, u32[]{:S(2)}) collective-permute-start(bf16[1024,1024]{1,0:T(8,128)(2,1)S(1)} %constant_dynamic-slice_fusion.1), channel_id=1, source_target_pairs={{0,1},{1,0},{2,3},{3,2},{4,5},{5,4},{6,7},{7,6},{8,9},{9,8},{10,11... | collective-permute-start | bytes 6291464 | tf_op jit(solution)/shard_map/ppermute | solution.py:75
  398.3 1.6 constant_dynamic-slice_fusion
  399.9 1.6 collective-permute-start.3
  401.5 2.7 multiply_convert_fusion
  404.2 4.3 fusion.11
  408.5 3.4 collective-permute-start.1
  411.9 1.5 convert_bitcast_fusion
  413.5 3.3 fusion.21
  416.7 1.3 fusion.19
  418.1 4.3 fusion.25
  422.4 3.9 fusion.26
  (42 shorter events, 0.5 us)
Async XLA Ops:
  7.2 130.7 %copy-start = (bf16[1,512,2048]{2,1,0:T(8,128)(2,1)S(1)}, bf16[1,512,2048]{2,1,0:T(8,128)(2,1)}, u32[]{:S(2)}) copy-start(bf16[1,512,2048]{2,1,0:T(8,128)(2,1)} %param.15) | copy-start | bytes 6291460
  7.2 7.1 %copy-start.6 = (bf16[256,128]{1,0:T(8,128)(2,1)S(1)}, bf16[256,128]{1,0:T(8,128)(2,1)}, u32[]{:S(2)}) copy-start(bf16[256,128]{1,0:T(8,128)(2,1)} %param.16) | copy-start | bytes 196612
  7.2 79.8 %all-gather.3.cloned.1.call-start = ((), (), s32[]{:S(2)}) async-start(), calls=%async_computation.5 | async-start | bytes 1114112 | tf_op jit(solution)/shard_map/all_gather | solution.py:153
  13.1 8.3 %copy-start.7 = (s32[256,2]{0,1:T(2,128)S(1)}, s32[256,2]{0,1:T(2,128)}, u32[]{:S(2)}) copy-start(s32[256,2]{0,1:T(2,128)} %param.12) | copy-start | bytes 6148
  13.1 9.2 %copy-start.8 = (f32[256,2]{0,1:T(2,128)S(1)}, f32[256,2]{0,1:T(2,128)}, u32[]{:S(2)}) copy-start(f32[256,2]{0,1:T(2,128)} %param.13) | copy-start | bytes 6148
  15.5 14.1 %all-to-all-start = ((bf16[8,256,128]{2,1,0:T(8,128)(2,1)}), bf16[8,256,128]{2,1,0:T(8,128)(2,1)}, u32[]{:S(2)}, u32[]{:S(2)}) async-start(bf16[8,256,128]{2,1,0:T(8,128)(2,1)} %pad_maximum_fusion), calls=%async_computation | async-start | bytes 1048576 | tf_op jit(solution)/shard_map/all_to_all | solution.py:65
  21.3 218.4 %reduce-scatter.3.cloned.1.call-start = ((), (), s32[]{:S(2)}) async-start(), calls=%async_computation.6 | async-start | bytes 2359296 | tf_op jit(solution)/shard_map/reduce_scatter | solution.py:33
  199.2 190.3 %all-gather.5.cloned.1.call-start = ((), (), s32[]{:S(2)}) async-start(), calls=%async_computation.8 | async-start | bytes 8912896 | tf_op jit(solution)/shard_map/all_gather | solution.py:167
  199.9 212.0 %reduce-scatter.5.cloned.1.call-start = ((), (), s32[]{:S(2)}) async-start(), calls=%async_computation.7 | async-start | bytes 393216 | tf_op jit(solution)/shard_map/reduce_scatter | solution.py:33
  389.5 12.0 %copy-start.9 = (bf16[1,2048,512]{2,1,0:T(8,128)(2,1)S(1)}, bf16[1,2048,512]{2,1,0:T(8,128)(2,1)}, u32[]{:S(2)}) copy-start(bf16[1,2048,512]{2,1,0:T(8,128)(2,1)} %param.20) | copy-start | bytes 6291460
  393.6 4.7 %copy-start.2 = (bf16[1024,2048]{1,0:T(8,128)(2,1)}, bf16[1024,2048]{1,0:T(8,128)(2,1)S(1)}, u32[]{:S(2)}) copy-start(bf16[1024,2048]{1,0:T(8,128)(2,1)S(1)} %get-tuple-element.9) | copy-start | bytes 12582916
  393.6 10.6 %copy-start.4 = (bf16[1024,2048]{1,0:T(8,128)(2,1)}, bf16[1024,2048]{1,0:T(8,128)(2,1)S(1)}, u32[]{:S(2)}) copy-start(bf16[1024,2048]{1,0:T(8,128)(2,1)S(1)} %get-tuple-element.10) | copy-start | bytes 12582916
  393.6 7.9 %copy-start.5 = (bf16[2048,2048]{1,0:T(8,128)(2,1)S(1)}, bf16[2048,2048]{1,0:T(8,128)(2,1)}, u32[]{:S(2)}) copy-start(bf16[2048,2048]{1,0:T(8,128)(2,1)} %all-gather.5.cloned.1.call-done) | copy-start | bytes 25165828
  393.9 24.2 %collective-permute-start = (bf16[1024,1024]{1,0:T(8,128)(2,1)S(1)}, bf16[1024,1024]{1,0:T(8,128)(2,1)}, u32[]{:S(2)}, u32[]{:S(2)}) collective-permute-start(bf16[1024,1024]{1,0:T(8,128)(2,1)S(1)} %constant_dynamic-slice_fusion.1), channel_id=1, source_target_pairs={{0,1},{1,0},{2,3},{3,2},{4,5},{5,4},{6,7},{7,6},{8,9},{9,8},{10,11... | collective-permute-start | bytes 6291464 | tf_op jit(solution)/shard_map/ppermute | solution.py:75
  399.9 4.4 %copy-start.10 = (bf16[1,512,2048]{2,1,0:T(8,128)(2,1)S(1)}, bf16[1,512,2048]{2,1,0:T(8,128)(2,1)}, u32[]{:S(2)}) copy-start(bf16[1,512,2048]{2,1,0:T(8,128)(2,1)} %param.21) | copy-start | bytes 6291460
  399.9 22.5 %collective-permute-start.3 = (bf16[1024,1024]{1,0:T(8,128)(2,1)}, bf16[1024,1024]{1,0:T(8,128)(2,1)}, u32[]{:S(2)}, u32[]{:S(2)}) collective-permute-start(bf16[1024,1024]{1,0:T(8,128)(2,1)} %constant_dynamic-slice_fusion), channel_id=1, source_target_pairs={{0,1},{1,0},{2,3},{3,2},{4,5},{5,4},{6,7},{7,6},{8,9},{9,8},{10,11... | collective-permute-start | bytes 6291464 | tf_op jit(solution)/shard_map/ppermute | solution.py:75
  408.5 9.5 %collective-permute-start.1 = (bf16[1024,512]{1,0:T(8,128)(2,1)}, bf16[1024,512]{1,0:T(8,128)(2,1)}, u32[]{:S(2)}, u32[]{:S(2)}) collective-permute-start(bf16[1024,512]{1,0:T(8,128)(2,1)} %fusion.11), channel_id=1, source_target_pairs={{0,1},{1,0},{2,3},{3,2},{4,5},{5,4},{6,7},{7,6},{8,9},{9,8},{10,11... | collective-permute-start | bytes 3145736 | tf_op jit(solution)/shard_map/ppermute | solution.py:75
  413.4 3.3 copy-start.3
  413.4 8.9 %collective-permute-start.2 = (bf16[1024,512]{1,0:T(8,128)(2,1)S(1)}, bf16[1024,512]{1,0:T(8,128)(2,1)S(1)}, u32[]{:S(2)}, u32[]{:S(2)}) collective-permute-start(bf16[1024,512]{1,0:T(8,128)(2,1)S(1)} %get-tuple-element.13), channel_id=1, source_target_pairs={{0,1},{1,0},{2,3},{3,2},{4,5},{5,4},{6,7},{7,6},{8,9},{9,8},{10,11... | collective-permute-start | bytes 3145736 | tf_op jit(solution)/shard_map/ppermute | solution.py:75
  418.1 8.1 %copy-start.1 = (bf16[1,512,2048]{2,1,0:T(8,128)(2,1)S(1)}, bf16[1,512,2048]{2,1,0:T(8,128)(2,1)}, u32[]{:S(2)}) copy-start(bf16[1,512,2048]{2,1,0:T(8,128)(2,1)} %param.15) | copy-start | bytes 6291460
Sparse Core Ops, SparseCore 0:
  10.5 76.4 all-gather.2
  199.3 40.3 reduce-scatter.2
  242.8 146.6 all-gather.4
  391.8 17.8 reduce-scatter.4
where the time goes:
time: 433 us
  waiting for transfers between devices  252 us (58%)
  blocking collectives  94.8 us (22%)
  matrix products  35.9 us (8%)
  starting transfers between devices  15.4 us (4%)
  between operations  14 us (3%)
  local copies, waits for them, and re-layouts  12.1 us (3%)
  other arithmetic  8.19 us (2%)
    all_gather x1, waiting for transfers between devices, on_device(): both = lax.all_gather(both, TENSOR, axis=1, tiled=True)  150 us
    all_gather x1, waiting for transfers between devices, on_device(): whole = lax.all_gather(x_real, TENSOR, axis=1, tiled=True)  55.5 us
    all_to_all x1, blocking collectives, on_device(): lax.all_to_all(sent, 'expert', split_axis=0, concat_axis=0, tiled=True)  48.2 us
    all_to_all x1, blocking collectives, on_device(): lax.all_to_all(partial_out.reshape(experts, capacity, width), 'expert', s...  46.6 us
    reduce_scatter x2, waiting for transfers between devices, reduced_to_own(): pieces = lax.psum_scatter(pieces, axes[k], scatter_dimension=0, tiled=True)  39.7 us
    dot_general x4, matrix products, over_rows(): lax.dot_general(left, right, (((0,), (0,)), ((), ())), preferred_element_...  12.7 us
    dot_general x1, matrix products, on_device(): jnp.dot(hidden, w_down, preferred_element_type=jnp.float32)  9.62 us
    ppermute x4, starting transfers between devices, partner(): return lax.ppermute(value, axis, pairs)  9.43 us
  transfers between devices with their start and end apart: 9, of which 4 were waited for; matrix products, arithmetic and copies ran while one was open for 8% of the time, Pallas kernels for 0%

commit v1 on v0

--- a/solution.py
+++ b/solution.py
@@ -150,7 +150,9 @@
     wf_down = down_fake[0]
     real_pos = slot_index(routes_real, experts, capacity)
     real_pick = spread_matrix(real_pos, total)
-    whole = lax.all_gather(x_real, TENSOR, axis=1, tiled=True)
+    whole = jnp.concatenate(
+        lax.all_to_all(jnp.stack([x_real] * lax.axis_size(TENSOR)), TENSOR, 0, 0), axis=1
+    )
     fake_pos = slot_index(routes_fake, experts, capacity)
     fake_pick = spread_matrix(fake_pos, total)
     fake_flat = pick_matrix(fake_pos, total)

time: 433 us -> 386 us (0.89)
  waiting for transfers between devices: 252 us -> 185 us
  starting transfers between devices: 15.4 us -> 26.3 us
  blocking collectives: 94.8 us -> 100 us
    all_gather x1 -> x0, waiting for transfers between devices: 55.5 us -> none  [on_device(): whole = lax.all_gather(x_real, TENSOR, axis=1, tiled=True)]
    all_gather x1, waiting for transfers between devices: 150 us -> 103 us  [on_device(): both = lax.all_gather(both, TENSOR, axis=1, tiled=True)]
    all_to_all x0 -> x1, waiting for transfers between devices: none -> 21 us  [on_device(): lax.all_to_all(jnp.stack([x_real] * lax.axis_size(TENSOR)), TENSOR, 0, 0)]
    reduce_scatter x2, waiting for transfers between devices: 39.7 us -> 52.3 us  [reduced_to_own(): pieces = lax.psum_scatter(pieces, axes[k], scatter_dimension=0, tiled=True)]
    all_to_all x0 -> x1, starting transfers between devices: none -> 10.6 us  [on_device(): lax.all_to_all(jnp.stack([x_real] * lax.axis_size(TENSOR)), TENSOR, 0, 0)]
  transfers between devices with their start and end apart: 9 -> 9, of which waited for: 4 -> 4; matrix products, arithmetic and copies ran while one was open for 8% -> 7% of each run, Pallas kernels for 0% -> 0%
where the time goes in v1:
time: 386 us; the launch traced here: 385 us
  waiting for transfers between devices  185 us (48%)
  blocking collectives  100 us (26%)
  matrix products  36.4 us (9%)
  starting transfers between devices  26.3 us (7%)
  between operations  15.8 us (4%)
  local copies, waits for them, and re-layouts  13.3 us (3%)
  other arithmetic  8.71 us (2%)
    all_gather x1, waiting for transfers between devices, on_device(): both = lax.all_gather(both, TENSOR, axis=1, tiled=True)  103 us
    reduce_scatter x2, waiting for transfers between devices, reduced_to_own(): pieces = lax.psum_scatter(pieces, axes[k], scatter_dimension=0, tiled=True)  52.3 us
    all_to_all x1, blocking collectives, on_device(): lax.all_to_all(sent, 'expert', split_axis=0, concat_axis=0, tiled=True)  50.6 us
    all_to_all x1, blocking collectives, on_device(): lax.all_to_all(partial_out.reshape(experts, capacity, width), 'expert', s...  49.3 us
    all_to_all x1, waiting for transfers between devices, on_device(): lax.all_to_all(jnp.stack([x_real] * lax.axis_size(TENSOR)), TENSOR, 0, 0)  21 us
    dot_general x4, matrix products, over_rows(): lax.dot_general(left, right, (((0,), (0,)), ((), ())), preferred_element_...  12.7 us
    all_to_all x1, starting transfers between devices, on_device(): lax.all_to_all(jnp.stack([x_real] * lax.axis_size(TENSOR)), TENSOR, 0, 0)  10.6 us
    dot_general x1, matrix products, on_device(): jnp.dot(hidden, w_down, preferred_element_type=jnp.float32)  9.62 us
  transfers between devices with their start and end apart: 9, of which 4 were waited for; matrix products, arithmetic and copies ran while one was open for 7% of the time, Pallas kernels for 0%

profile of v1, /device:TPU:1, one launch (start us, length us, event | category | flops | bytes accessed | tf_op | source)
XLA Modules:
  0.0 385.4 jit_solution(541823334545403023)
XLA Ops:
  8.0 0.8 convert_reduce_fusion.2
  8.9 0.6 reduce-window.16
  9.4 0.2 slice_reduce_fusion
  9.8 0.7 select_reduce_fusion.1
  10.5 0.7 multiply_add_fusion.2
  11.3 0.3 convert_reduce_fusion
  11.6 0.1 eq.86
  11.7 0.8 copy.33
  12.5 0.1 mul.132
  12.7 1.2 convolution_convert_fusion.2
  13.9 0.9 mul.134
  14.8 0.9 fusion.31
  15.7 0.8 pad_maximum_fusion
  16.5 6.0 %all-to-all-start.1 = ((bf16[8,256,128]{2,1,0:T(8,128)(2,1)}), bf16[8,256,128]{2,1,0:T(8,128)(2,1)S(1)}, u32[]{:S(2)}, u32[]{:S(2)}) async-start(bf16[8,256,128]{2,1,0:T(8,128)(2,1)} %pad_maximum_fusion), calls=%async_computation.1 | async-start | bytes 1048576 | tf_op jit(solution)/shard_map/all_to_all | solution.py:65
  22.6 8.6 %all-to-all-done.1 = bf16[8,256,128]{2,1,0:T(8,128)(2,1)S(1)} async-done(((bf16[8,256,128]{2,1,0:T(8,128)(2,1)}), bf16[8,256,128]{2,1,0:T(8,128)(2,1)S(1)}, u32[]{:S(2)}, u32[]{:S(2)}) %all-to-all-start.1) | async-done | bytes 524320 | tf_op jit(solution)/shard_map/all_to_all | solution.py:65
  31.2 1.1 stack.2
  32.4 10.6 %all-to-all-start = ((bf16[16,256,128]{1,2,0:T(8,128)(2,1)}), bf16[16,256,128]{1,2,0:T(8,128)(2,1)S(1)}, u32[]{:S(2)}, u32[]{:S(2)}) async-start(bf16[16,256,128]{1,2,0:T(8,128)(2,1)} %stack.2), calls=%async_computation | async-start | bytes 2097152 | tf_op jit(solution)/shard_map/all_to_all | solution.py:154
  43.1 0.6 reduce-window.14
  43.7 0.2 slice_reduce_fusion.1
  44.1 1.6 select_reduce_fusion
  45.6 1.1 fusion.50
  46.7 0.9 pad_maximum_fusion.1
  47.6 21.0 %all-to-all-done = bf16[16,256,128]{1,2,0:T(8,128)(2,1)S(1)} async-done(((bf16[16,256,128]{1,2,0:T(8,128)(2,1)}), bf16[16,256,128]{1,2,0:T(8,128)(2,1)S(1)}, u32[]{:S(2)}, u32[]{:S(2)}) %all-to-all-start) | async-done | bytes 1048608 | tf_op jit(solution)/shard_map/all_to_all | solution.py:154
  68.6 2.4 convolution_convert_fusion.1
  71.0 50.6 %all_to_all.20 = bf16[8,128,2048]{2,1,0:T(8,128)(2,1)} all-to-all(bf16[8,128,2048]{2,1,0:T(8,128)(2,1)S(1)} %bitcast.75), channel_id=1, replica_groups=mesh['expert'=8,'tensor_0'=2,'tensor_1'=8,'dp'=2] {'expert'}, dimensions={0} | all-to-all | bytes 8388608 | tf_op jit(solution)/shard_map/all_to_all | solution.py:173
  121.6 9.6 %convolution_convert_fusion = bf16[1024,2048]{1,0:T(8,128)(2,1)} fusion(bf16[1,512,2048]{2,1,0:T(8,128)(2,1)S(1)} %copy-done, bf16[1024,2048]{1,0:T(8,128)(2,1)} %bitcast.81, bf16[1,2048,512]{2,1,0:T(8,128)(2,1)} %param.14), kind=kOutput, calls=%fused_computation | convolution fusion | flops 4301783040 | bytes 12582912 | tf_op jit(solution)/shard_map/dot_general | solution.py:177
  131.2 49.3 %all_to_all.21 = bf16[8,128,2048]{2,1,0:T(8,128)(2,1)S(1)} all-to-all(bf16[8,128,2048]{2,1,0:T(8,128)(2,1)} %bitcast.82), channel_id=1, replica_groups=mesh['expert'=8,'tensor_0'=2,'tensor_1'=8,'dp'=2] {'expert'}, dimensions={0} | all-to-all | bytes 8388608 | tf_op jit(solution)/shard_map/all_to_all | solution.py:178
  180.6 1.3 fusion.38
  181.8 1.3 fusion.24
  183.2 0.4 copy.35
  183.6 2.0 copy.34
  185.7 0.5 all-gather.2.cloned.1.call-update
  186.2 0.2 reduce-scatter.5.cloned.1.call-start
  186.4 52.3 %reduce-scatter.3.cloned.1.call-done = f32[2,256,128]{2,1,0:T(8,128)} async-done(((f32[16,256,128]{2,1,0:T(8,128)}), f32[2,256,128]{2,1,0:T(8,128)}) %reduce-scatter.3.cloned.1.call-update) | async-done | bytes 262160 | tf_op jit(solution)/shard_map/reduce_scatter | solution.py:33
  238.8 102.5 %all-gather.2.cloned.1.call-done = bf16[2048,2048]{1,0:T(8,128)(2,1)} async-done(((bf16[2048,128]{1,0:T(8,128)(2,1)}), bf16[2048,2048]{1,0:T(8,128)(2,1)}) %all-gather.2.cloned.1.call-update) | async-done | bytes 8388624 | tf_op jit(solution)/shard_map/all_gather | solution.py:169
  341.3 4.1 %fusion.49 = (bf16[1024,2048]{1,0:T(8,128)(2,1)S(1)}, bf16[1024,2048]{1,0:T(8,128)(2,1)S(1)}) fusion(bf16[2048,2048]{1,0:T(8,128)(2,1)} %all-gather.2.cloned.1.call-done), kind=kLoop, calls=%fused_computation.78 | loop fusion | bytes 16777216 | tf_op jit(solution)/shard_map/slice | solution.py:170
  345.4 0.2 constant_dynamic-slice_fusion.1
  345.7 4.3 %collective-permute-start = (bf16[1024,1024]{1,0:T(8,128)(2,1)S(1)}, bf16[1024,1024]{1,0:T(8,128)(2,1)}, u32[]{:S(2)}, u32[]{:S(2)}) collective-permute-start(bf16[1024,1024]{1,0:T(8,128)(2,1)S(1)} %constant_dynamic-slice_fusion.1), channel_id=1, source_target_pairs={{0,1},{1,0},{2,3},{3,2},{4,5},{5,4},{6,7},{7,6},{8,9},{9,8},{10,11... | collective-permute-start | bytes 6291464 | tf_op jit(solution)/shard_map/ppermute | solution.py:75
  349.9 1.6 constant_dynamic-slice_fusion
  351.5 1.8 collective-permute-start.3
  353.3 2.7 multiply_convert_fusion
  356.1 4.3 %fusion.11 = bf16[1024,512]{1,0:T(8,128)(2,1)} fusion(f32[1024,512]{1,0:T(8,128)S(1)} %get-tuple-element.14, bf16[1,512,2048]{2,1,0:T(8,128)(2,1)S(1)} %copy-done.12, bf16[2048,2048]{1,0:T(8,128)(2,1)S(1)} %copy-done.5), kind=kOutput, calls=%fused_computation.17 | convolution fusion | flops 2157445120 | bytes 9437184 | tf_op jit(solution)/shard_map/dot_general | solution.py:196
  360.3 3.3 collective-permute-start.1
  363.6 1.5 convert_bitcast_fusion
  365.2 3.3 fusion.21
  368.5 1.3 fusion.19
  369.8 4.3 %fusion.25 = bf16[1,1024,512]{2,1,0:T(8,128)(2,1)} fusion(f32[1024,512]{1,0:T(8,128)S(1)} %fusion.21, bf16[1024,1024]{1,0:T(8,128)(2,1)} %collective-permute-done, bf16[1024,512]{1,0:T(8,128)(2,1)} %collective-permute-done.1), kind=kOutput, calls=%fused_computation.40 | convolution fusion | flops 1074790400 | bytes 6291456 | tf_op jit(solution)/shard_map/dot_general | solution.py:119
  374.1 3.9 %fusion.26 = bf16[1,512,1024]{2,1,0:T(8,128)(2,1)} fusion(f32[512,1024]{1,0:T(8,128)S(1)} %fusion.19, bf16[1024,512]{1,0:T(8,128)(2,1)S(1)} %collective-permute-done.2, bf16[1024,1024]{1,0:T(8,128)(2,1)} %collective-permute-done.3), kind=kOutput, calls=%fused_computation.41 | convolution fusion | flops 1074790400 | bytes 6291456 | tf_op jit(solution)/shard_map/dot_general | solution.py:119
  (47 shorter events, 0.7 us)
Async XLA Ops:
  8.0 113.6 %copy-start = (bf16[1,512,2048]{2,1,0:T(8,128)(2,1)S(1)}, bf16[1,512,2048]{2,1,0:T(8,128)(2,1)}, u32[]{:S(2)}) copy-start(bf16[1,512,2048]{2,1,0:T(8,128)(2,1)} %param.15) | copy-start | bytes 6291460
  12.7 9.9 %copy-start.8 = (bf16[256,128]{1,0:T(8,128)(2,1)S(1)}, bf16[256,128]{1,0:T(8,128)(2,1)}, u32[]{:S(2)}) copy-start(bf16[256,128]{1,0:T(8,128)(2,1)} %param.11) | copy-start | bytes 196612
  16.5 26.5 %copy-start.9 = (s32[256,2]{0,1:T(2,128)S(1)}, s32[256,2]{0,1:T(2,128)}, u32[]{:S(2)}) copy-start(s32[256,2]{0,1:T(2,128)} %param.12) | copy-start | bytes 6148
  16.5 27.5 %copy-start.10 = (f32[256,2]{0,1:T(2,128)S(1)}, f32[256,2]{0,1:T(2,128)}, u32[]{:S(2)}) copy-start(f32[256,2]{0,1:T(2,128)} %param.13) | copy-start | bytes 6148
  16.5 14.7 %all-to-all-start.1 = ((bf16[8,256,128]{2,1,0:T(8,128)(2,1)}), bf16[8,256,128]{2,1,0:T(8,128)(2,1)S(1)}, u32[]{:S(2)}, u32[]{:S(2)}) async-start(bf16[8,256,128]{2,1,0:T(8,128)(2,1)} %pad_maximum_fusion), calls=%async_computation.1 | async-start | bytes 1048576 | tf_op jit(solution)/shard_map/all_to_all | solution.py:65
  31.2 1.1 copy-start.7
  32.4 36.2 %all-to-all-start = ((bf16[16,256,128]{1,2,0:T(8,128)(2,1)}), bf16[16,256,128]{1,2,0:T(8,128)(2,1)S(1)}, u32[]{:S(2)}, u32[]{:S(2)}) async-start(bf16[16,256,128]{1,2,0:T(8,128)(2,1)} %stack.2), calls=%async_computation | async-start | bytes 2097152 | tf_op jit(solution)/shard_map/all_to_all | solution.py:154
  43.0 195.7 %reduce-scatter.3.cloned.1.call-start = ((), (), s32[]{:S(2)}) async-start(), calls=%async_computation.6 | async-start | bytes 2359296 | tf_op jit(solution)/shard_map/reduce_scatter | solution.py:33
  131.2 49.3 %copy-start.6 = (f32[256,1024]{1,0:T(8,128)S(1)}, f32[256,1024]{1,0:T(8,128)}, u32[]{:S(2)}) copy-start(f32[256,1024]{1,0:T(8,128)} %get-tuple-element.7) | copy-start | bytes 3145732
  185.6 155.7 %all-gather.2.cloned.1.call-start = ((), (), s32[]{:S(2)}) async-start(), calls=%async_computation.8 | async-start | bytes 8912896 | tf_op jit(solution)/shard_map/all_gather | solution.py:169
  186.2 177.4 %reduce-scatter.5.cloned.1.call-start = ((), (), s32[]{:S(2)}) async-start(), calls=%async_computation.7 | async-start | bytes 393216 | tf_op jit(solution)/shard_map/reduce_scatter | solution.py:33
  341.3 12.0 %copy-start.11 = (bf16[1,2048,512]{2,1,0:T(8,128)(2,1)S(1)}, bf16[1,2048,512]{2,1,0:T(8,128)(2,1)}, u32[]{:S(2)}) copy-start(bf16[1,2048,512]{2,1,0:T(8,128)(2,1)} %param.20) | copy-start | bytes 6291460
  345.4 4.5 %copy-start.2 = (bf16[1024,2048]{1,0:T(8,128)(2,1)}, bf16[1024,2048]{1,0:T(8,128)(2,1)S(1)}, u32[]{:S(2)}) copy-start(bf16[1024,2048]{1,0:T(8,128)(2,1)S(1)} %get-tuple-element.9) | copy-start | bytes 12582916
  345.4 10.6 %copy-start.4 = (bf16[1024,2048]{1,0:T(8,128)(2,1)}, bf16[1024,2048]{1,0:T(8,128)(2,1)S(1)}, u32[]{:S(2)}) copy-start(bf16[1024,2048]{1,0:T(8,128)(2,1)S(1)} %get-tuple-element.10) | copy-start | bytes 12582916
  345.4 7.9 %copy-start.5 = (bf16[2048,2048]{1,0:T(8,128)(2,1)S(1)}, bf16[2048,2048]{1,0:T(8,128)(2,1)}, u32[]{:S(2)}) copy-start(bf16[2048,2048]{1,0:T(8,128)(2,1)} %all-gather.2.cloned.1.call-done) | copy-start | bytes 25165828
  345.7 24.1 %collective-permute-start = (bf16[1024,1024]{1,0:T(8,128)(2,1)S(1)}, bf16[1024,1024]{1,0:T(8,128)(2,1)}, u32[]{:S(2)}, u32[]{:S(2)}) collective-permute-start(bf16[1024,1024]{1,0:T(8,128)(2,1)S(1)} %constant_dynamic-slice_fusion.1), channel_id=1, source_target_pairs={{0,1},{1,0},{2,3},{3,2},{4,5},{5,4},{6,7},{7,6},{8,9},{9,8},{10,11... | collective-permute-start | bytes 6291464 | tf_op jit(solution)/shard_map/ppermute | solution.py:75
  351.5 4.5 %copy-start.12 = (bf16[1,512,2048]{2,1,0:T(8,128)(2,1)S(1)}, bf16[1,512,2048]{2,1,0:T(8,128)(2,1)}, u32[]{:S(2)}) copy-start(bf16[1,512,2048]{2,1,0:T(8,128)(2,1)} %param.21) | copy-start | bytes 6291460
  351.5 22.6 %collective-permute-start.3 = (bf16[1024,1024]{1,0:T(8,128)(2,1)}, bf16[1024,1024]{1,0:T(8,128)(2,1)}, u32[]{:S(2)}, u32[]{:S(2)}) collective-permute-start(bf16[1024,1024]{1,0:T(8,128)(2,1)} %constant_dynamic-slice_fusion), channel_id=1, source_target_pairs={{0,1},{1,0},{2,3},{3,2},{4,5},{5,4},{6,7},{7,6},{8,9},{9,8},{10,11... | collective-permute-start | bytes 6291464 | tf_op jit(solution)/shard_map/ppermute | solution.py:75
  360.3 9.4 %collective-permute-start.1 = (bf16[1024,512]{1,0:T(8,128)(2,1)}, bf16[1024,512]{1,0:T(8,128)(2,1)}, u32[]{:S(2)}, u32[]{:S(2)}) collective-permute-start(bf16[1024,512]{1,0:T(8,128)(2,1)} %fusion.11), channel_id=1, source_target_pairs={{0,1},{1,0},{2,3},{3,2},{4,5},{5,4},{6,7},{7,6},{8,9},{9,8},{10,11... | collective-permute-start | bytes 3145736 | tf_op jit(solution)/shard_map/ppermute | solution.py:75
  365.2 3.3 copy-start.3
  365.2 8.9 %collective-permute-start.2 = (bf16[1024,512]{1,0:T(8,128)(2,1)S(1)}, bf16[1024,512]{1,0:T(8,128)(2,1)S(1)}, u32[]{:S(2)}, u32[]{:S(2)}) collective-permute-start(bf16[1024,512]{1,0:T(8,128)(2,1)S(1)} %get-tuple-element.13), channel_id=1, source_target_pairs={{0,1},{1,0},{2,3},{3,2},{4,5},{5,4},{6,7},{7,6},{8,9},{9,8},{10,11... | collective-permute-start | bytes 3145736 | tf_op jit(solution)/shard_map/ppermute | solution.py:75
  369.8 8.1 %copy-start.1 = (bf16[1,512,2048]{2,1,0:T(8,128)(2,1)S(1)}, bf16[1,512,2048]{2,1,0:T(8,128)(2,1)}, u32[]{:S(2)}) copy-start(bf16[1,512,2048]{2,1,0:T(8,128)(2,1)} %param.15) | copy-start | bytes 6291460
Sparse Core Ops, SparseCore 0:
  185.7 52.9 reduce-scatter.2
  241.2 22.5 reduce-scatter.4
Sparse Core Ops, SparseCore 1:
  188.6 152.6 all-gather.1
